TPU v7x, 32 devices: a whole 2x2x4 slice. The times are simulated.
32 devices in a mesh: prow: 4 (over y, core), pcol: 8 (over z, x).
Axes of the slice: x: 2, y: 2, z: 4, core: 2. Of those that a mesh axis runs over, the one named last changes fastest.
Arguments:
- vectors: bfloat16 [512, 120064], P('pcol', 'prow'), may hold values from -6 to 6
- reflectors: bfloat16 [2, 256, 120064], P(None, 'pcol', 'prow'), may hold values from -6 to 6
- panel_factor: float32 [2, 256, 256], replicated, as said below
Outputs:
- band_vectors: bfloat16 [8, 64, 120064], P('pcol', 'prow')
Inputs may be any that keep to these rules, and one draw needn't show every extreme that they name: `panel_factor`: upper triangular: zero below the diagonal; diagonal entries between 1 / 120064 and 3 / 120064.
All inputs are finite; a program needn't handle non-finite values.
Results may differ from a plain program's by a relative error of at most 0.0095.
Values may be sent and summed in bfloat16 or wider, within the bound.
A program may use at most 192 MiB of HBM per device.

v0:
```python
import functools

import jax
import jax.numpy as jnp
from jax import lax
from jax.experimental import pallas as pl
from jax.experimental.pallas import tpu as pltpu
from jax.sharding import PartitionSpec as P

MESH = pl.DeviceIdType.MESH
LANES = 128
SPLIT = 4
F32, BF16 = jnp.float32, jnp.bfloat16
NT = (((1,), (1,)), ((), ()))


def kernel(
    n_row, n_col, main, k_block, out_blocks,
    v_ref, w_ref, vx_ref, wx_ref, t_ref, o_ref,
    v_s, w_s, part, rs_send, rs_recv, ag, s_s,
    v_send, v_recv, w_send, w_recv, r_send, r_recv, g_send, g_recv, o_send, o_recv, l_sem,
):
    me_r, me_c = lax.axis_index("prow"), lax.axis_index("pcol")
    me_a, me_b = lax.rem(me_c, SPLIT), lax.div(me_c, SPLIT)
    halves, group = n_col // SPLIT, SPLIT * n_row
    me_g = me_a * n_row + me_r
    width = v_s.shape[2]
    rows = SPLIT * v_s.shape[1]
    panel = w_s.shape[1] * w_s.shape[2]
    own = v_s.shape[1] // n_row
    middle = width // 2
    pieces = ((0, middle), (middle, main), (main, main + LANES))

    def remote(src, dst, send, recv, r, c):
        return pltpu.make_async_remote_copy(
            src_ref=src, dst_ref=dst, send_sem=send, recv_sem=recv,
            device_id={"prow": r, "pcol": c}, device_id_type=MESH,
        )

    def source(number, q):
        start, stop = pieces[number]
        if start == main:
            return pl.ds(pl.multiple_of(q * LANES, LANES), LANES)
        return pl.ds(pl.multiple_of(q * main + start, LANES), stop - start)

    def move(kind, number, b, q, c, here):
        start, stop = pieces[number]
        target = pl.ds(start, stop - start)
        if kind == "v":
            src = (vx_ref if start == main else v_ref).at[:, source(number, q)]
            slot, sent, come, mine, theirs = (
                lambda a: v_s.at[a, :, target], v_send, v_recv, me_a, q
            )
        else:
            src = (wx_ref if start == main else w_ref).at[:, :, source(number, q)]
            slot, sent, come, mine, theirs = (
                lambda a: w_s.at[:, a, :, target], w_send, w_recv, me_c, c
            )
        if here:
            copy = pltpu.make_async_copy(src, slot(mine), l_sem.at[number, 0 if kind == "v" else 1])
            copy.start()
            local[number].append(copy)
            return
        copy = remote(src, slot(mine), sent.at[number, theirs], come.at[number, mine], me_r, c)
        copy.start()
        sends.append(copy)
        arrivals[number].append(
            remote(src, slot(theirs), sent.at[number, theirs], come.at[number, theirs], me_r, c)
        )

    sends, arrivals, local = [], [[], [], []], [[], [], []]
    for number in (0, 2, 1):
        near, far = [], []
        for ka in reversed(range(SPLIT)):
            q = lax.rem(me_a + ka, SPLIT)
            near.append(("v", number, me_b, q, me_b * SPLIT + q, ka == 0))
            near.append(("w", number, me_b, q, me_b * SPLIT + q, ka == 0))
        for kb in reversed(range(1, halves)):
            b = lax.rem(me_b + kb, halves)
            for ka in reversed(range(SPLIT)):
                q = lax.rem(me_a + ka + 2 * me_r, SPLIT)
                far.append(("w", number, b, q, b * SPLIT + q, False))
        for at in range(max(len(near), len(far))):
            for order in (near, far):
                if at < len(order):
                    move(*order[at])
    if width > main + LANES:
        pad = width - main - LANES
        v_s[:, :, main + LANES:] = jnp.zeros((SPLIT, v_s.shape[1], pad), BF16)
        w_s[:, :, :, main + LANES:] = jnp.zeros((2, n_col, w_s.shape[2], pad), BF16)
    part[...] = jnp.zeros_like(part)

    def panel_of(p, cols):
        block = w_s[p, :, :, cols]
        if w_s.shape[2] % 16:
            block = block.astype(F32)
        return block.reshape(panel, block.shape[-1]).astype(BF16)

    def products(begin, end):
        @pl.loop(begin // k_block, end // k_block)
        def _(i):
            cols = pl.ds(pl.multiple_of(i * k_block, k_block), k_block)
            v = v_s[:, :, cols].reshape(rows, k_block)
            first, second = panel_of(0, cols), panel_of(1, cols)
            part[:, :panel] += lax.dot_general(v, first, NT, preferred_element_type=F32)
            part[:, panel:2 * panel] += lax.dot_general(v, second, NT, preferred_element_type=F32)
            part[:, 2 * panel:] += lax.dot_general(first, second, NT, preferred_element_type=F32)

    def landed(number):
        for copy in local[number]:
            copy.wait()
        for copy in arrivals[number]:
            copy.wait_recv()

    landed(0)
    products(0, middle)
    landed(2)
    landed(1)
    products(middle, width)

    rs_send[...] = part[...].astype(BF16).reshape(rs_send.shape)
    partners = [lax.rem(me_g + k, group) for k in range(1, group)]

    def place(g):
        return lax.rem(g, n_row), me_b * SPLIT + lax.div(g, n_row)

    got = []
    for g in partners:
        copy = remote(rs_send.at[g], rs_recv.at[me_g], r_send.at[g], r_recv.at[me_g], *place(g))
        copy.start()
        sends.append(copy)
        got.append(remote(rs_send.at[g], rs_recv.at[g], r_send.at[g], r_recv.at[g], *place(g)))
    total = rs_send[me_g].astype(F32)
    for g, copy in zip(partners, got):
        copy.wait_recv()
        total += rs_recv[g].astype(F32)
    ag[me_g] = total.astype(BF16)
    got = []
    for g in partners:
        copy = remote(ag.at[me_g], ag.at[me_g], g_send.at[g], g_recv.at[me_g], *place(g))
        copy.start()
        sends.append(copy)
        got.append(remote(ag.at[me_g], ag.at[g], g_send.at[g], g_recv.at[g], *place(g)))
    for copy in got:
        copy.wait_recv()

    sums = ag[...].reshape(rows, 3 * panel)
    high = lax.Precision.HIGHEST
    s1 = lax.dot_general(
        sums[:, :panel].astype(F32), t_ref[0], NT, precision=high, preferred_element_type=F32
    ).astype(BF16)
    p2 = sums[:, panel:2 * panel].astype(F32) - jnp.dot(
        s1, sums[:, 2 * panel:], preferred_element_type=F32
    )
    s2 = lax.dot_general(p2, t_ref[1], NT, precision=high, preferred_element_type=F32).astype(BF16)
    s_s[0] = s1
    s_s[1] = s2

    n_block = 2 * LANES
    got = []

    def hand_out(j, start, size):
        def piece(g):
            r = lax.rem(g, n_row)
            return v_s.at[
                lax.div(g, n_row), pl.ds(pl.multiple_of(r * own, own), own), pl.ds(start, size)
            ]

        def landing(g):
            a = lax.div(g, n_row)
            at = SPLIT * main + a * LANES if start == main else a * main + start
            return o_ref.at[lax.rem(g, n_row), :, pl.ds(pl.multiple_of(at, LANES), size)]

        for g in partners:
            copy = remote(piece(g), landing(me_g), o_send.at[g, j], o_recv.at[me_g, j], *place(g))
            copy.start()
            sends.append(copy)
            got.append(
                remote(piece(g), landing(g), o_send.at[g, j], o_recv.at[g, j], *place(g)).wait_recv
            )
        copy = pltpu.make_async_copy(piece(me_g), landing(me_g), o_send.at[me_g, j])
        copy.start()
        got.append(copy.wait)

    for j, (start, stop) in enumerate(out_blocks):

        @pl.loop(start // n_block, stop // n_block)
        def _(i):
            cols = pl.ds(pl.multiple_of(i * n_block, n_block), n_block)
            v = v_s[:, :, cols].reshape(rows, n_block).astype(F32)
            v = v - jnp.dot(s_s[0], panel_of(0, cols), preferred_element_type=F32)
            v = v - jnp.dot(s_s[1], panel_of(1, cols), preferred_element_type=F32)
            v_s[:, :, cols] = v.astype(BF16).reshape(SPLIT, rows // SPLIT, n_block)

        hand_out(j, start, min(stop, main) - start)
        if stop > main:
            hand_out(len(out_blocks), main, LANES)
    for wait in got:
        wait()
    for copy in sends:
        copy.wait_send()


def lay_out(columns, in_ref, out_ref):
    for r in range(in_ref.shape[0]):
        out_ref[:, r * columns:(r + 1) * columns] = in_ref[r, :, :columns]


def body(n_row, n_col, vectors, reflectors, panel_factor):
    own_rows, columns = vectors.shape
    panel = panel_factor.shape[1]
    main = columns // (SPLIT * LANES) * LANES
    covered = SPLIT * main
    k_block = 6 * LANES
    width = -(-(main + LANES) // (2 * k_block)) * 2 * k_block
    n_block = 2 * LANES
    extra = SPLIT * LANES - (columns - covered)
    v_x = jnp.pad(vectors[:, covered:], ((0, 0), (0, extra)))
    w_x = jnp.pad(reflectors[:, :, covered:], ((0, 0), (0, 0), (0, extra)))
    group = SPLIT * n_row
    rows = SPLIT * own_rows
    step = -(-width // n_block // 6) * n_block
    out_blocks = [(s, min(s + step, width)) for s in range(0, width, step)]
    out_count = len(out_blocks) + 1
    dma = pltpu.SemaphoreType.DMA
    received = pl.pallas_call(
        functools.partial(kernel, n_row, n_col, main, k_block, out_blocks),
        out_shape=jax.ShapeDtypeStruct(
            (n_row, own_rows // n_row, covered + SPLIT * LANES), BF16
        ),
        in_specs=[pl.BlockSpec(memory_space=pl.ANY)] * 4
        + [pl.BlockSpec(memory_space=pltpu.VMEM)],
        out_specs=pl.BlockSpec(memory_space=pl.ANY),
        scratch_shapes=[
            pltpu.VMEM((SPLIT, own_rows, width), BF16),
            pltpu.VMEM((2, n_col, reflectors.shape[1], width), BF16),
            pltpu.VMEM((rows, 3 * panel), F32),
            pltpu.VMEM((group, rows // group, 3 * panel), BF16),
            pltpu.VMEM((group, rows // group, 3 * panel), BF16),
            pltpu.VMEM((group, rows // group, 3 * panel), BF16),
            pltpu.VMEM((2, rows, panel), BF16),
            dma((3, SPLIT)), dma((3, SPLIT)), dma((3, n_col)), dma((3, n_col)),
            dma((group,)), dma((group,)), dma((group,)), dma((group,)),
            dma((group, out_count)), dma((group, out_count)), dma((3, 2)),
        ],
        compiler_params=pltpu.CompilerParams(
            has_side_effects=True, vmem_limit_bytes=56 * 1024 * 1024
        ),
        name="panels",
    )(vectors, reflectors, v_x, w_x, panel_factor)
    whole = pl.pallas_call(
        functools.partial(lay_out, columns),
        out_shape=jax.ShapeDtypeStruct((own_rows // n_row, n_row * columns), BF16),
        in_specs=[pl.BlockSpec(memory_space=pltpu.VMEM)],
        out_specs=pl.BlockSpec(memory_space=pltpu.VMEM),
        compiler_params=pltpu.CompilerParams(vmem_limit_bytes=24 * 1024 * 1024),
        name="lay_out",
    )(received)
    return whole[None]


def solution(mesh):
    placed = (P("pcol", "prow"), P(None, "pcol", "prow"), P())
    return jax.shard_map(
        functools.partial(body, mesh.shape["prow"], mesh.shape["pcol"]),
        mesh=mesh, in_specs=placed, out_specs=P("pcol", "prow", None), check_vma=False,
    )
```

profile of v0, /device:TPU:0, one launch (start us, length us, event | category | flops | bytes accessed | tf_op | source)
XLA Modules:
  0.0 265.6 jit_solution(4488055569958931962)
XLA Ops:
  0.0 0.8 slice.6
  0.8 0.6 pad.8.vx_ref
  1.4 0.8 slice.7
  2.2 0.6 pad.9.wx_ref
  2.9 258.2 %panels.1.in_ref = bf16[4,16,30208]{2,1,0:T(8,128)(2,1)} custom-call(bf16[64,30016]{1,0:T(8,128)(2,1)} %v_ref.1, bf16[2,32,30016]{2,1,0:T(8,128)(2,1)} %w_ref.1, bf16[64,512]{1,0:T(8,128)(2,1)} %pad.8.vx_ref, bf16[2,32,512]{2,1,0:T(8,128)(2,1)} %pad.9.wx_ref, f32[2,256,256]{2,1,0:T(8,128)} %t_ref.1), custom_call_target="tpu_custom_call" | custom-call | tf_op jit(solution)/shard_map/panels/pallas_call | solution.py:226
  261.0 0.0 copy-start
  261.0 2.1 copy-done
  263.1 2.5 lay_out.1
Async XLA Ops:
  261.0 2.1 copy-start
where the time goes:
time: 266 us
  Pallas kernels  261 us (98%)
  local copies, waits for them, and re-layouts  4.95 us (2%)
    pallas_call x1, Pallas kernels, body(): pl.pallas_call(functools.partial(kernel, n_row, n_col, main, k_block, out...  258 us

commit v1 on v0

v1 whole, which is shorter than its diff:
```python
import functools

import jax
import jax.numpy as jnp
from jax import lax
from jax.experimental import pallas as pl
from jax.experimental.pallas import tpu as pltpu
from jax.sharding import PartitionSpec as P

MESH = pl.DeviceIdType.MESH
LANES = 128
SPLIT = 4
F32, BF16 = jnp.float32, jnp.bfloat16
NT = (((1,), (1,)), ((), ()))


def flip(index, bit):
    return index + bit - 2 * bit * lax.rem(lax.div(index, bit), 2)


def flipped(index, mask):
    bit = 1
    while bit <= mask:
        if mask & bit:
            index = flip(index, bit)
        bit *= 2
    return index


def kernel(
    n_row, n_col, columns, plan,
    v_ref, w_ref, vt_ref, wt_ref, t_ref, o_ref,
    v_s, w_s, v_mid, w_mid, v_tail, w_tail, part, rs_send, rs_recv, ag, s_s, stage,
    vx_send, wx_send, v_send, w_send, v_recv, w_recv, m_recv,
    r_send, r_recv, g_send, g_recv, o_send, o_recv, l_sem,
):
    site, main, rest, pieces, sums_at, out_blocks, n_block = plan
    me_r, me_c = lax.axis_index("prow"), lax.axis_index("pcol")
    me_a, me_b = lax.rem(me_c, SPLIT), lax.div(me_c, SPLIT)
    halves, group = n_col // SPLIT, SPLIT * n_row
    me_g = me_a * n_row + me_r
    rows = SPLIT * v_s.shape[1]
    panel = w_s.shape[1] * w_s.shape[2]
    own = v_s.shape[1] // n_row
    side_c, side_a = flip(me_c, 1), flip(me_a, 1)
    far_a = flip(me_a, 2)
    others = [lax.rem(me_b + k, halves) for k in range(1, halves)]

    def turns(mask):
        a, r = mask // n_row, mask % n_row
        first = 0 if a & 2 else 1 if a & 1 else 2 if r > 1 else 3
        size = -(bool(a & 1) * 2 + (r > 1)) if first == 0 else (r > 1)
        return first, size, mask

    masks = sorted(range(1, group), key=turns)

    def partner(mask):
        a, r = flipped(me_a, mask // n_row), flipped(me_r, mask % n_row)
        return a * n_row + r, r, me_b * SPLIT + a

    partners = [partner(mask) for mask in masks]

    barrier = pltpu.get_barrier_semaphore()
    for _, r, c in partners:
        pl.semaphore_signal(barrier, device_id={"prow": r, "pcol": c}, device_id_type=MESH)
    for b in others:
        for a in (me_a, far_a):
            pl.semaphore_signal(
                barrier, device_id={"prow": me_r, "pcol": b * SPLIT + a}, device_id_type=MESH
            )
    pl.semaphore_wait(barrier, len(partners) + 2 * len(others))

    def remote(src, dst, send, recv, r, c):
        return pltpu.make_async_remote_copy(
            src_ref=src, dst_ref=dst, send_sem=send, recv_sem=recv,
            device_id={"prow": r, "pcol": c}, device_id_type=MESH,
        )

    sends = []

    def start(copies, last):
        if len(copies) == 1:
            copies[0].start()
        else:
            pl.when(last)(copies[1].start)
            pl.when(jnp.logical_not(last))(copies[0].start)
        return copies[-1]

    def sources(full, tail, q, at, stop):
        cols = pl.ds(pl.multiple_of(q * site + at, LANES), stop - at)
        found = [full.at[..., cols]]
        if at == main:
            found.append(tail)
        return found

    def send(full, tail, q, number, dst, sent, come, c):
        at, stop = pieces[number]
        copies = [
            remote(src, dst, sent, come, me_r, c) for src in sources(full, tail, q, at, stop)
        ]
        sends.append(start(copies, q == SPLIT - 1))

    def keep(full, tail, q, number, dst, sem):
        at, stop = pieces[number]
        copies = [pltpu.make_async_copy(src, dst, sem) for src in sources(full, tail, q, at, stop)]
        return start(copies, q == SPLIT - 1)

    def cols_of(number):
        at, stop = pieces[number]
        return pl.ds(at, stop - at)

    def along(number, v_from, w_here, w_there, a, c, send_at):
        cols, n = cols_of(number), send_at
        for b in others:
            w_here(number, b * SPLIT + me_a, w_s.at[:, c, :, cols], w_send.at[number, n], w_recv.at[number, c])
            n += 1
            w_there(number, b * SPLIT + far_a, w_s.at[:, c, :, cols], w_send.at[number, n], w_recv.at[number, c])
            n += 1
        to = me_b * SPLIT + far_a
        v_from(number, to, v_s.at[a, :, cols], v_send.at[number, send_at and 1], v_recv.at[number, a])
        w_there(number, to, w_s.at[:, c, :, cols], w_send.at[number, n], w_recv.at[number, c])

    v_tail[...] = jnp.zeros_like(v_tail)
    w_tail[...] = jnp.zeros_like(w_tail)
    if rest:
        v_tail[:, :rest] = vt_ref[:, :rest]
        w_tail[:, :, :rest] = wt_ref[:, :, :rest]
    width = v_s.shape[2]
    if width > site:
        v_s[:, :, site:] = jnp.zeros((SPLIT, v_s.shape[1], width - site), BF16)
        w_s[:, :, :, site:] = jnp.zeros((2, n_col, w_s.shape[2], width - site), BF16)
    part[...] = jnp.zeros_like(part)

    def from_v(q):
        return lambda number, c, dst, sent, come: send(v_ref, v_tail, q, number, dst, sent, come, c)

    def from_w(q):
        return lambda number, c, dst, sent, come: send(w_ref, w_tail, q, number, dst, sent, come, c)

    side_far = flip(side_a, 2)
    local = []
    for number in range(len(pieces)):
        cols = cols_of(number)
        w_first = from_w(side_far)
        w_first(number, side_c, w_mid.at[:, :, cols], wx_send.at[number, 0], m_recv.at[number, 0])
        from_v(side_far)(number, side_c, v_mid.at[:, cols], vx_send.at[number, 0], m_recv.at[number, 1])
        from_w(side_a)(
            number, side_c, w_s.at[:, me_c, :, cols], wx_send.at[number, 1], w_recv.at[number, me_c]
        )
        from_v(side_a)(
            number, side_c, v_s.at[me_a, :, cols], vx_send.at[number, 1], v_recv.at[number, me_a]
        )
        along(number, from_v(far_a), from_w(me_a), from_w(far_a), me_a, me_c, 0)
        local.append((
            keep(v_ref, v_tail, me_a, number, v_s.at[me_a, :, cols], l_sem.at[number, 0]),
            keep(w_ref, w_tail, me_a, number, w_s.at[:, me_c, :, cols], l_sem.at[number, 1]),
        ))

    def come(dst, sem):
        remote(dst, dst, sem, sem, me_r, side_c).wait_recv()

    def passed_on(src):
        def start_copy(number, c, dst, sent, recv):
            copy = remote(src(number), dst, sent, recv, me_r, c)
            copy.start()
            sends.append(copy)
        return start_copy

    for number in range(len(pieces)):
        cols = cols_of(number)
        come(w_mid.at[:, :, cols], m_recv.at[number, 0])
        come(v_mid.at[:, cols], m_recv.at[number, 1])
        come(w_s.at[:, side_c, :, cols], w_recv.at[number, side_c])
        come(v_s.at[side_a, :, cols], v_recv.at[number, side_a])
        along(
            number,
            passed_on(lambda n: v_mid.at[:, cols_of(n)]),
            passed_on(lambda n: w_s.at[:, side_c, :, cols_of(n)]),
            passed_on(lambda n: w_mid.at[:, :, cols_of(n)]),
            side_a, side_c, 2 * halves - 1,
        )

    def panel_of(p, cols):
        block = w_s[p, :, :, cols]
        if w_s.shape[2] % 16:
            block = block.astype(F32)
        return block.reshape(panel, block.shape[-1]).astype(BF16)

    def products(at, stop):
        cols = pl.ds(at, stop - at)
        v = v_s[:, :, cols].reshape(rows, stop - at)
        first, second = panel_of(0, cols), panel_of(1, cols)
        part[:, :panel] += lax.dot_general(v, first, NT, preferred_element_type=F32)
        part[:, panel:2 * panel] += lax.dot_general(v, second, NT, preferred_element_type=F32)
        part[:, 2 * panel:] += lax.dot_general(first, second, NT, preferred_element_type=F32)

    for number in range(len(pieces)):
        cols = cols_of(number)
        for copy in local[number]:
            copy.wait()
        for a in (far_a, side_far):
            come(v_s.at[a, :, cols], v_recv.at[number, a])
        for b in [me_b] + others:
            for a in (me_a, side_a, far_a, side_far):
                if b is me_b and (a is me_a or a is side_a):
                    continue
                c = b * SPLIT + a
                come(w_s.at[:, c, :, cols], w_recv.at[number, c])
        products(*sums_at[number])

    rs_send[...] = part[...].astype(BF16).reshape(rs_send.shape)
    for g, r, c in partners:
        copy = remote(rs_send.at[g], rs_recv.at[me_g], r_send.at[g], r_recv.at[me_g], r, c)
        copy.start()
        sends.append(copy)
    total = rs_send[me_g].astype(F32)
    for g, r, c in reversed(partners):
        remote(rs_send.at[g], rs_recv.at[g], r_send.at[g], r_recv.at[g], r, c).wait_recv()
        total += rs_recv[g].astype(F32)
    ag[me_g] = total.astype(BF16)
    for g, r, c in partners:
        copy = remote(ag.at[me_g], ag.at[me_g], g_send.at[g], g_recv.at[me_g], r, c)
        copy.start()
        sends.append(copy)
    for g, r, c in partners:
        remote(ag.at[me_g], ag.at[g], g_send.at[g], g_recv.at[g], r, c).wait_recv()

    sums = ag[...].reshape(rows, 3 * panel)
    high = lax.Precision.HIGHEST
    s1 = lax.dot_general(
        sums[:, :panel].astype(F32), t_ref[0], NT, precision=high, preferred_element_type=F32
    ).astype(BF16)
    p2 = sums[:, panel:2 * panel].astype(F32) - jnp.dot(
        s1, sums[:, 2 * panel:], preferred_element_type=F32
    )
    s2 = lax.dot_general(p2, t_ref[1], NT, precision=high, preferred_element_type=F32).astype(BF16)
    s_s[0] = s1
    s_s[1] = s2

    def piece(a, r, at, size):
        return v_s.at[a, pl.ds(pl.multiple_of(r * own, own), own), pl.ds(at, size)]

    def landing(a, r, at, size):
        return stage.at[r, :, pl.ds(pl.multiple_of(a * site + at, LANES), size)]

    for j, (at, stop) in enumerate(out_blocks):

        @pl.loop(at // n_block, stop // n_block)
        def _(i):
            cols = pl.ds(pl.multiple_of(i * n_block, n_block), n_block)
            v = v_s[:, :, cols].reshape(rows, n_block).astype(F32)
            v = v - jnp.dot(s_s[0], panel_of(0, cols), preferred_element_type=F32)
            v = v - jnp.dot(s_s[1], panel_of(1, cols), preferred_element_type=F32)
            v_s[:, :, cols] = v.astype(BF16).reshape(SPLIT, rows // SPLIT, n_block)

        size = min(stop, site) - at
        for g, r, c in partners:
            a = lax.div(g, n_row)
            copy = remote(
                piece(a, r, at, size), landing(me_a, me_r, at, size),
                o_send.at[g, j], o_recv.at[me_g, j], r, c,
            )
            copy.start()
            sends.append(copy)

    for j, (at, stop) in enumerate(out_blocks):
        size = min(stop, site) - at
        stage[me_r, :, pl.ds(pl.multiple_of(me_a * site + at, LANES), size)] = v_s[
            me_a, pl.ds(pl.multiple_of(me_r * own, own), own), pl.ds(at, size)
        ]
        for g, r, c in partners:
            a = lax.div(g, n_row)
            remote(
                piece(a, r, at, size), landing(a, r, at, size), o_send.at[g, j], o_recv.at[g, j], r, c
            ).wait_recv()
        for r in range(n_row):
            for a in range(SPLIT):
                begin, end = a * site + at, min(a * site + at + size, columns)
                if end > begin:
                    o_ref[:, r * columns + begin:r * columns + end] = stage[r, :, begin:end]
    for copy in sends:
        copy.wait_send()


def body(n_row, n_col, vectors, reflectors, panel_factor):
    own_rows, columns = vectors.shape
    part_rows, panel = reflectors.shape[1], panel_factor.shape[1]
    halves, group, rows = n_col // SPLIT, SPLIT * n_row, SPLIT * own_rows
    site = -(-columns // (SPLIT * LANES)) * LANES
    last = columns - (SPLIT - 1) * site
    main, rest = last // LANES * LANES, last % LANES
    n_block = 2 * LANES
    width = -(-site // n_block) * n_block
    step = -(-main // (4 * n_block)) * n_block
    cuts = list(range(0, main, step)) + [main]
    even = main // n_block * n_block
    pieces = tuple(zip(cuts[:-1], cuts[1:])) + ((main, site),)
    sums_at = tuple((s, min(e, even)) for s, e in pieces[:-1]) + ((even, width),)
    marks = [0, 2 * n_block]
    blocks = width // n_block
    marks += [n_block * (2 + (blocks - 2) * k // 6) for k in range(1, 7)]
    out_blocks = tuple(zip(marks[:-1], marks[1:]))
    edge = min(((SPLIT - 1) * site + main) // LANES, -(-columns // LANES) - 1)
    count, hops = len(pieces), 2 * (2 * halves - 1)
    dma = pltpu.SemaphoreType.DMA
    plan = (site, main, rest, pieces, sums_at, out_blocks, n_block)
    whole = pl.pallas_call(
        functools.partial(kernel, n_row, n_col, columns, plan),
        grid=(1,),
        out_shape=jax.ShapeDtypeStruct((own_rows // n_row, n_row * columns), BF16),
        in_specs=[
            pl.BlockSpec(memory_space=pl.ANY),
            pl.BlockSpec(memory_space=pl.ANY),
            pl.BlockSpec((own_rows, LANES), lambda i: (0, edge)),
            pl.BlockSpec((2, part_rows, LANES), lambda i: (0, 0, edge)),
            pl.BlockSpec(panel_factor.shape, lambda i: (0, 0, 0)),
        ],
        out_specs=pl.BlockSpec(memory_space=pltpu.VMEM),
        scratch_shapes=[
            pltpu.VMEM((SPLIT, own_rows, width), BF16),
            pltpu.VMEM((2, n_col, part_rows, width), BF16),
            pltpu.VMEM((own_rows, site), BF16),
            pltpu.VMEM((2, part_rows, site), BF16),
            pltpu.VMEM((own_rows, site - main), BF16),
            pltpu.VMEM((2, part_rows, site - main), BF16),
            pltpu.VMEM((rows, 3 * panel), F32),
            pltpu.VMEM((group, rows // group, 3 * panel), BF16),
            pltpu.VMEM((group, rows // group, 3 * panel), BF16),
            pltpu.VMEM((group, rows // group, 3 * panel), BF16),
            pltpu.VMEM((2, rows, panel), BF16),
            pltpu.VMEM((n_row, own_rows // n_row, SPLIT * site), BF16),
            dma((count, 2)), dma((count, 2)), dma((count, 2)), dma((count, hops)),
            dma((count, SPLIT)), dma((count, n_col)), dma((count, 2)),
            dma((group,)), dma((group,)), dma((group,)), dma((group,)),
            dma((group, len(out_blocks))), dma((group, len(out_blocks))), dma((count, 2)),
        ],
        compiler_params=pltpu.CompilerParams(
            has_side_effects=True, collective_id=0, vmem_limit_bytes=48 * 1024 * 1024
        ),
        name="panels",
    )(vectors, reflectors, vectors, reflectors, panel_factor)
    return whole[None]


def solution(mesh):
    placed = (P("pcol", "prow"), P(None, "pcol", "prow"), P())
    return jax.shard_map(
        functools.partial(body, mesh.shape["prow"], mesh.shape["pcol"]),
        mesh=mesh, in_specs=placed, out_specs=P("pcol", "prow", None), check_vma=False,
    )
```

time: 266 us -> 241 us (0.906)
  Pallas kernels: 261 us -> 238 us
    pallas_call x2 -> x1, Pallas kernels: 261 us -> 238 us  [body(): pl.pallas_call(functools.partial(kernel, n_row, n_col, columns, plan), gr...]
where the time goes in v1:
time: 241 us
  Pallas kernels  238 us (99%)
  local copies, waits for them, and re-layouts  2.94 us (1%)
    pallas_call x1, Pallas kernels, body(): pl.pallas_call(functools.partial(kernel, n_row, n_col, columns, plan), gr...  238 us

profile of v1, /device:TPU:0, one launch (start us, length us, event | category | flops | bytes accessed | tf_op | source)
XLA Modules:
  0.0 241.2 jit_solution(14374265263358345551)
XLA Ops:
  0.0 0.0 copy-start
  0.0 1.0 copy-done
  1.0 238.3 %panels.1 = bf16[16,120064]{1,0:T(8,128)(2,1)S(1)} custom-call(bf16[64,30016]{1,0:T(8,128)(2,1)} %vt_ref.1, bf16[2,32,30016]{2,1,0:T(8,128)(2,1)} %wt_ref.1, bf16[64,30016]{1,0:T(8,128)(2,1)} %vt_ref.1, bf16[2,32,30016]{2,1,0:T(8,128)(2,1)} %wt_ref.1, f32[2,256,256]{2,1,0:T(8,128)S(1)} %copy-done), custom_call_target="tpu_custom_call" | custom-call | tf_op jit(solution)/shard_map/panels/pallas_call | solution.py:307
  239.3 1.9 copy.5
Async XLA Ops:
  0.0 1.0 copy-start

commit v2 on v1

v2 whole, which is shorter than its diff:
```python
import functools

import jax
import jax.numpy as jnp
from jax import lax
from jax.experimental import pallas as pl
from jax.experimental.pallas import tpu as pltpu
from jax.sharding import PartitionSpec as P

MESH = pl.DeviceIdType.MESH
LANES = 128
SPLIT = 4
F32, BF16 = jnp.float32, jnp.bfloat16
NT = (((1,), (1,)), ((), ()))


def flip(index, bit):
    return index + bit - 2 * bit * lax.rem(lax.div(index, bit), 2)


def flipped(index, mask):
    bit = 1
    while bit <= mask:
        if mask & bit:
            index = flip(index, bit)
        bit *= 2
    return index


def kernel(
    n_row, n_col, columns, plan,
    v_ref, w_ref, vt_ref, wt_ref, t_ref, o_ref,
    v_s, w_s, v_mid, w_mid, v_tail, w_tail, t_s, part, rs_send, rs_recv, ag, s_s, stage,
    v_send, w_send, v_recv, w_recv, v_side, w_side, r_send, r_recv, g_send, g_recv,
    o_send, o_recv, l_sem, t_sem,
):
    site, main, rest, pieces, sums_at, out_blocks, n_block = plan
    me_r, me_c = lax.axis_index("prow"), lax.axis_index("pcol")
    me_a, me_b = lax.rem(me_c, SPLIT), lax.div(me_c, SPLIT)
    halves, group = n_col // SPLIT, SPLIT * n_row
    me_g = me_a * n_row + me_r
    rows = SPLIT * v_s.shape[1]
    panel = w_s.shape[1] * w_s.shape[2]
    own = v_s.shape[1] // n_row
    side_c, side_a = flip(me_c, 1), flip(me_a, 1)
    far_a, side_far = flip(me_a, 2), flip(side_a, 2)
    others = [lax.rem(me_b + k, halves) for k in range(1, halves)]

    def turns(mask):
        a, r = mask // n_row, mask % n_row
        first = 0 if a & 2 else 1 if a & 1 else 2 if r > 1 else 3
        size = -(bool(a & 1) * 2 + (r > 1)) if first == 0 else (r > 1)
        return first, size, mask

    masks = sorted(range(1, group), key=turns)

    def partner(mask):
        a, r = flipped(me_a, mask // n_row), flipped(me_r, mask % n_row)
        return a * n_row + r, r, me_b * SPLIT + a

    partners = [partner(mask) for mask in masks]

    barrier = pltpu.get_barrier_semaphore()
    for _, r, c in partners:
        pl.semaphore_signal(barrier, device_id={"prow": r, "pcol": c}, device_id_type=MESH)
    for b in others:
        for a in (me_a, far_a):
            pl.semaphore_signal(
                barrier, device_id={"prow": me_r, "pcol": b * SPLIT + a}, device_id_type=MESH
            )

    def remote(src, dst, send, recv, r, c):
        return pltpu.make_async_remote_copy(
            src_ref=src, dst_ref=dst, send_sem=send, recv_sem=recv,
            device_id={"prow": r, "pcol": c}, device_id_type=MESH,
        )

    def cols_of(number):
        at, stop = pieces[number]
        return pl.ds(at, stop - at)

    def start(make, full, tail, q, number):
        at, stop = pieces[number]
        copy = make(full.at[..., pl.ds(pl.multiple_of(q * site + at, LANES), stop - at)])
        if at == main:
            pl.when(q == SPLIT - 1)(make(tail).start)
            pl.when(q != SPLIT - 1)(copy.start)
        else:
            copy.start()

    def send(full, tail, q, dst, sent, come):
        def start_copy(number, c):
            start(
                lambda src: remote(src, dst(number), sent, come.at[number], me_r, c),
                full, tail, q, number,
            )
        return start_copy

    def pass_on(src, dst, sent, come):
        def start_copy(number, c):
            remote(src(number), dst(number), sent, come.at[number], me_r, c).start()
        return start_copy

    def v_slot(a):
        return lambda number: v_s.at[a, :, cols_of(number)]

    def w_slot(c):
        return lambda number: w_s.at[:, c, :, cols_of(number)]

    def v_half(number):
        return v_mid.at[:, cols_of(number)]

    def w_half(number):
        return w_mid.at[:, :, cols_of(number)]

    def along(number, v_there, w_here, w_there):
        for b in others:
            w_here(number, b * SPLIT + me_a)
            w_there(number, b * SPLIT + far_a)
        v_there(number, me_b * SPLIT + far_a)
        w_there(number, me_b * SPLIT + far_a)

    def wait(ref, sem):
        pltpu.make_async_copy(ref, ref, sem).wait()

    keep_t = pltpu.make_async_copy(t_ref, t_s, t_sem)
    keep_t.start()
    v_tail[...] = jnp.zeros_like(v_tail)
    w_tail[...] = jnp.zeros_like(w_tail)
    if rest:
        v_tail[:, :rest] = vt_ref[:, :rest]
        w_tail[:, :, :rest] = wt_ref[:, :, :rest]
    width = v_s.shape[2]
    if width > site:
        v_s[:, :, site:] = jnp.zeros((SPLIT, v_s.shape[1], width - site), BF16)
        w_s[:, :, :, site:] = jnp.zeros((2, n_col, w_s.shape[2], width - site), BF16)
    part[...] = jnp.zeros_like(part)
    pl.semaphore_wait(barrier, len(partners) + 2 * len(others))

    v_own, w_own = v_slot(me_a), w_slot(me_c)
    v_to = send(v_ref, v_tail, far_a, v_own, v_send, v_recv)
    w_stay = send(w_ref, w_tail, me_a, w_own, w_send, w_recv)
    w_to = send(w_ref, w_tail, far_a, w_own, w_send, w_recv)
    to_side = [
        send(w_ref, w_tail, side_far, w_half, w_send, w_side),
        send(v_ref, v_tail, side_far, v_half, v_send, v_side),
        send(w_ref, w_tail, side_a, w_own, w_send, w_side),
        send(v_ref, v_tail, side_a, v_own, v_send, v_side),
    ]
    for number in range(len(pieces)):
        along(number, v_to, w_stay, w_to)
        for copy in to_side:
            copy(number, side_c)
    for number in range(len(pieces)):
        for k, (full, tail, slot) in enumerate(((v_ref, v_tail, v_own), (w_ref, w_tail, w_own))):
            start(
                lambda src: pltpu.make_async_copy(src, slot(number), l_sem.at[number, k]),
                full, tail, me_a, number,
            )

    v_on = pass_on(v_half, v_slot(side_a), v_send, v_recv)
    w_stay_on = pass_on(w_slot(side_c), w_slot(side_c), w_send, w_recv)
    w_on = pass_on(w_half, w_slot(side_c), w_send, w_recv)
    for number in range(len(pieces)):
        wait(w_s.at[:, pl.ds(0, 2), :, cols_of(number)], w_side.at[number])
        wait(v_s.at[pl.ds(0, 2), :, cols_of(number)], v_side.at[number])
        along(number, v_on, w_stay_on, w_on)

    def panel_of(p, cols):
        block = w_s[p, :, :, cols]
        if w_s.shape[2] % 16:
            block = block.astype(F32)
        return block.reshape(panel, block.shape[-1]).astype(BF16)

    def products(at, stop):
        cols = pl.ds(at, stop - at)
        v = v_s[:, :, cols].reshape(rows, stop - at)
        first, second = panel_of(0, cols), panel_of(1, cols)
        part[:, :panel] += lax.dot_general(v, first, NT, preferred_element_type=F32)
        part[:, panel:2 * panel] += lax.dot_general(v, second, NT, preferred_element_type=F32)
        part[:, 2 * panel:] += lax.dot_general(first, second, NT, preferred_element_type=F32)

    for number in range(len(pieces)):
        wait(v_s.at[0, :, cols_of(number)], l_sem.at[number, 0])
        wait(w_s.at[:, 0, :, cols_of(number)], l_sem.at[number, 1])
        wait(v_s.at[pl.ds(0, 2), :, cols_of(number)], v_recv.at[number])
        wait(w_s.at[:, pl.ds(0, n_col - 2), :, cols_of(number)], w_recv.at[number])
        products(*sums_at[number])

    rs_send[...] = part[...].astype(BF16).reshape(rs_send.shape)
    for g, r, c in partners:
        remote(rs_send.at[g], rs_recv.at[me_g], r_send, r_recv, r, c).start()
    rs_recv[me_g] = rs_send[me_g]
    wait(rs_recv.at[pl.ds(0, group - 1)], r_recv)
    ag[me_g] = jnp.sum(rs_recv[...].astype(F32), axis=0).astype(BF16)
    for g, r, c in partners:
        remote(ag.at[me_g], ag.at[me_g], g_send, g_recv, r, c).start()
    keep_t.wait()
    wait(ag.at[pl.ds(0, group - 1)], g_recv)

    sums = ag[...].reshape(rows, 3 * panel)
    high = lax.Precision.HIGHEST
    s1 = lax.dot_general(
        sums[:, :panel].astype(F32), t_s[0], NT, precision=high, preferred_element_type=F32
    ).astype(BF16)
    p2 = sums[:, panel:2 * panel].astype(F32) - jnp.dot(
        s1, sums[:, 2 * panel:], preferred_element_type=F32
    )
    s2 = lax.dot_general(p2, t_s[1], NT, precision=high, preferred_element_type=F32).astype(BF16)
    s_s[0] = s1
    s_s[1] = s2

    def rows_of(r):
        return pl.ds(pl.multiple_of(r * own, own), own)

    for j, (at, stop) in enumerate(out_blocks):

        @pl.loop(at // n_block, stop // n_block)
        def _(i):
            cols = pl.ds(pl.multiple_of(i * n_block, n_block), n_block)
            v = v_s[:, :, cols].reshape(rows, n_block).astype(F32)
            v = v - jnp.dot(s_s[0], panel_of(0, cols), preferred_element_type=F32)
            v = v - jnp.dot(s_s[1], panel_of(1, cols), preferred_element_type=F32)
            v_s[:, :, cols] = v.astype(BF16).reshape(SPLIT, rows // SPLIT, n_block)

        cols = pl.ds(at, min(stop, site) - at)
        for g, r, c in partners:
            remote(
                v_s.at[lax.div(g, n_row), rows_of(r), cols], stage.at[me_g, :, cols],
                o_send, o_recv.at[j], r, c,
            ).start()

    for j, (at, stop) in enumerate(out_blocks):
        size = min(stop, site) - at
        cols = pl.ds(at, size)
        stage[me_g, :, cols] = v_s[me_a, rows_of(me_r), cols]
        wait(stage.at[pl.ds(0, group - 1), :, cols], o_recv.at[j])
        for r in range(n_row):
            for a in range(SPLIT):
                size = min(at + size, columns - a * site) - at
                begin = r * columns + a * site + at
                if size > 0:
                    o_ref[:, begin:begin + size] = stage[a * n_row + r, :, at:at + size]
                size = min(stop, site) - at
    wait(v_s.at[:, :, pl.ds(0, site)], v_send)
    wait(w_s.at[:, :, :, pl.ds(0, site)], w_send)
    wait(rs_recv.at[pl.ds(0, group - 1)], r_send)
    wait(ag.at[pl.ds(0, group - 1)], g_send)
    wait(stage.at[pl.ds(0, group - 1)], o_send)


def body(n_row, n_col, vectors, reflectors, panel_factor):
    own_rows, columns = vectors.shape
    part_rows, panel = reflectors.shape[1], panel_factor.shape[1]
    halves, group, rows = n_col // SPLIT, SPLIT * n_row, SPLIT * own_rows
    site = -(-columns // (SPLIT * LANES)) * LANES
    last = columns - (SPLIT - 1) * site
    main, rest = last // LANES * LANES, last % LANES
    n_block = 2 * LANES
    width = -(-site // n_block) * n_block
    step = -(-main // (4 * n_block)) * n_block
    cuts = list(range(0, main, step)) + [main]
    even = main // n_block * n_block
    pieces = tuple(zip(cuts[:-1], cuts[1:])) + ((main, site),)
    sums_at = tuple((s, min(e, even)) for s, e in pieces[:-1]) + ((even, width),)
    marks = [0, 2 * n_block]
    blocks = width // n_block
    marks += [n_block * (2 + (blocks - 2) * k // 6) for k in range(1, 7)]
    out_blocks = tuple(zip(marks[:-1], marks[1:]))
    edge = min(((SPLIT - 1) * site + main) // LANES, -(-columns // LANES) - 1)
    count = len(pieces)
    dma = pltpu.SemaphoreType.DMA
    plan = (site, main, rest, pieces, sums_at, out_blocks, n_block)
    whole = pl.pallas_call(
        functools.partial(kernel, n_row, n_col, columns, plan),
        grid=(1,),
        out_shape=jax.ShapeDtypeStruct((own_rows // n_row, n_row * columns), BF16),
        in_specs=[
            pl.BlockSpec(memory_space=pl.ANY),
            pl.BlockSpec(memory_space=pl.ANY),
            pl.BlockSpec((own_rows, LANES), lambda i: (0, edge)),
            pl.BlockSpec((2, part_rows, LANES), lambda i: (0, 0, edge)),
            pl.BlockSpec(memory_space=pltpu.HBM),
        ],
        out_specs=pl.BlockSpec(memory_space=pltpu.VMEM),
        scratch_shapes=[
            pltpu.VMEM((SPLIT, own_rows, width), BF16),
            pltpu.VMEM((2, n_col, part_rows, width), BF16),
            pltpu.VMEM((own_rows, site), BF16),
            pltpu.VMEM((2, part_rows, site), BF16),
            pltpu.VMEM((own_rows, site - main), BF16),
            pltpu.VMEM((2, part_rows, site - main), BF16),
            pltpu.VMEM(panel_factor.shape, F32),
            pltpu.VMEM((rows, 3 * panel), F32),
            pltpu.VMEM((group, rows // group, 3 * panel), BF16),
            pltpu.VMEM((group, rows // group, 3 * panel), BF16),
            pltpu.VMEM((group, rows // group, 3 * panel), BF16),
            pltpu.VMEM((2, rows, panel), BF16),
            pltpu.VMEM((group, own_rows // n_row, site), BF16),
            dma, dma, dma((count,)), dma((count,)), dma((count,)), dma((count,)), dma, dma, dma, dma,
            dma, dma((len(out_blocks),)), dma((count, 2)), dma,
        ],
        compiler_params=pltpu.CompilerParams(
            has_side_effects=True, collective_id=0, vmem_limit_bytes=48 * 1024 * 1024
        ),
        name="panels",
    )(
        vectors, reflectors, vectors, reflectors,
        pltpu.with_memory_space_constraint(panel_factor, pltpu.HBM),
    )
    return whole[None]


def solution(mesh):
    placed = (P("pcol", "prow"), P(None, "pcol", "prow"), P())
    return jax.shard_map(
        functools.partial(body, mesh.shape["prow"], mesh.shape["pcol"]),
        mesh=mesh, in_specs=placed, out_specs=P("pcol", "prow", None), check_vma=False,
    )
```

time: 241 us -> 237 us (0.983)
  Pallas kernels: 238 us -> 234 us
    pallas_call x1, Pallas kernels: 238 us -> 234 us  [body(): pl.pallas_call(functools.partial(kernel, n_row, n_col, columns, plan), gr...]
where the time goes in v2:
time: 237 us; the launch traced here: 236 us
  Pallas kernels  234 us (99%)
    pallas_call x1, Pallas kernels, body(): pl.pallas_call(functools.partial(kernel, n_row, n_col, columns, plan), gr...  234 us

profile of v2, /device:TPU:0, one launch (start us, length us, event | category | flops | bytes accessed | tf_op | source)
XLA Modules:
  0.0 236.4 jit_solution(10719366510482433631)
XLA Ops:
  0.0 234.5 %panels.1 = bf16[16,120064]{1,0:T(8,128)(2,1)S(1)} custom-call(bf16[64,30016]{1,0:T(8,128)(2,1)} %vt_ref.1, bf16[2,32,30016]{2,1,0:T(8,128)(2,1)} %wt_ref.1, bf16[64,30016]{1,0:T(8,128)(2,1)} %vt_ref.1, bf16[2,32,30016]{2,1,0:T(8,128)(2,1)} %wt_ref.1, f32[2,256,256]{2,1,0:T(8,128)} %t_ref.1), custom_call_target="tpu_custom_call" | custom-call | tf_op jit(solution)/shard_map/panels/pallas_call | solution.py:274
  234.5 1.9 copy.5

commit v3 on v2

v3 whole, which is shorter than its diff:
```python
import functools

import jax
import jax.numpy as jnp
from jax import lax
from jax.experimental import pallas as pl
from jax.experimental.pallas import tpu as pltpu
from jax.sharding import PartitionSpec as P

MESH = pl.DeviceIdType.MESH
LANES = 128
SPLIT = 4
F32, BF16 = jnp.float32, jnp.bfloat16
NT = (((1,), (1,)), ((), ()))


def flip(index, bit):
    return index + bit - 2 * bit * lax.rem(lax.div(index, bit), 2)


def flipped(index, mask):
    bit = 1
    while bit <= mask:
        if mask & bit:
            index = flip(index, bit)
        bit *= 2
    return index


def kernel(
    n_row, n_col, columns, plan,
    v_ref, w_ref, vt_ref, wt_ref, t_ref, o_ref,
    v_s, w_s, v_mid, w_mid, v_tail, w_tail, t_s, part, s_s, stage,
    m_send, m_recv, z_send, z_recv, m_all, rs_send, rs_recv, ag,
    v_sent, w_sent, v_came, w_came, v_side, w_side, l_sem, t_sem,
    m_sems, r_send, r_recv, g_send, g_recv, o_send, o_recv,
):
    site, main, rest, pieces, sums_at, out_blocks, n_block, early = plan
    me_r, me_c = lax.axis_index("prow"), lax.axis_index("pcol")
    me_a, me_b = lax.rem(me_c, SPLIT), lax.div(me_c, SPLIT)
    me_x, me_e = lax.rem(me_a, 2), lax.div(me_a, 2)
    halves, group, plane = n_col // SPLIT, SPLIT * n_row, 2 * n_row
    me_g, me_h = me_a * n_row + me_r, me_x * n_row + me_r
    inner = lax.rem(me_b + me_e, 2) == 1
    rows = SPLIT * v_s.shape[1]
    panel = w_s.shape[1] * w_s.shape[2]
    own = v_s.shape[1] // n_row
    side_c, side_a = flip(me_c, 1), flip(me_a, 1)
    far_a, side_far = flip(me_a, 2), flip(side_a, 2)
    far_c = me_b * SPLIT + far_a
    others = [lax.rem(me_b + k, halves) for k in range(1, halves)]
    numbers = range(len(pieces))

    def turns(mask):
        a, r = mask // n_row, mask % n_row
        first = 0 if a & 2 else 1 if a & 1 else 2 if r > 1 else 3
        size = -(bool(a & 1) * 2 + (r > 1)) if first == 0 else (r > 1)
        return first, size, mask

    def partner(mask):
        a, r = flipped(me_a, mask // n_row), flipped(me_r, mask % n_row)
        return a * n_row + r, r, me_b * SPLIT + a

    partners = [partner(mask) for mask in sorted(range(1, group), key=turns)]
    near_by = [partner(mask) for mask in sorted(range(1, plane), key=turns)]

    barrier = pltpu.get_barrier_semaphore()
    for _, r, c in partners:
        pl.semaphore_signal(barrier, device_id={"prow": r, "pcol": c}, device_id_type=MESH)
    for b in others:
        for a in (me_a, far_a):
            pl.semaphore_signal(
                barrier, device_id={"prow": me_r, "pcol": b * SPLIT + a}, device_id_type=MESH
            )

    def remote(src, dst, send, recv, r, c):
        return pltpu.make_async_remote_copy(
            src_ref=src, dst_ref=dst, send_sem=send, recv_sem=recv,
            device_id={"prow": r, "pcol": c}, device_id_type=MESH,
        )

    def wait(ref, sem):
        pltpu.make_async_copy(ref, ref, sem).wait()

    def cols_of(number):
        at, stop = pieces[number]
        return pl.ds(at, stop - at)

    def start(make, full, tail, q, number):
        at, stop = pieces[number]
        copy = make(full.at[..., pl.ds(pl.multiple_of(q * site + at, LANES), stop - at)])
        if at == main:
            pl.when(q == SPLIT - 1)(make(tail).start)
            pl.when(q != SPLIT - 1)(copy.start)
        else:
            copy.start()

    def v_slot(a):
        return lambda number: v_s.at[a, :, cols_of(number)]

    def w_slot(p, c):
        return lambda number: w_s.at[p, c, :, cols_of(number)]

    def v_half(number):
        return v_mid.at[:, cols_of(number)]

    def w_half(p):
        return lambda number: w_mid.at[p, :, cols_of(number)]

    def send_v(q, dst, come):
        def start_copy(number, c):
            start(
                lambda src: remote(src, dst(number), v_sent, come.at[number], me_r, c),
                v_ref, v_tail, q, number,
            )
        return start_copy

    def send_w(p, q, dst, come):
        def start_copy(number, c):
            start(
                lambda src: remote(src, dst(number), w_sent, come.at[p, number], me_r, c),
                w_ref.at[p], w_tail.at[p], q, number,
            )
        return start_copy

    def pass_v(src, dst):
        def start_copy(number, c):
            remote(src(number), dst(number), v_sent, v_came.at[number], me_r, c).start()
        return start_copy

    def pass_w(p, src, dst):
        def start_copy(number, c):
            remote(src(number), dst(number), w_sent, w_came.at[p, number], me_r, c).start()
        return start_copy

    keep_t = pltpu.make_async_copy(t_ref, t_s, t_sem)
    keep_t.start()
    v_tail[...] = jnp.zeros_like(v_tail)
    w_tail[...] = jnp.zeros_like(w_tail)
    if rest:
        v_tail[:, :rest] = vt_ref[:, :rest]
        w_tail[:, :, :rest] = wt_ref[:, :, :rest]
    width = v_s.shape[2]
    if width > site:
        v_s[:, :, site:] = jnp.zeros((SPLIT, v_s.shape[1], width - site), BF16)
        w_s[:, :, :, site:] = jnp.zeros((2, n_col, w_s.shape[2], width - site), BF16)
    part[...] = jnp.zeros_like(part)
    pl.semaphore_wait(barrier, len(partners) + 2 * len(others))

    v_own = v_slot(me_a)
    near_v = send_v(far_a, v_own, v_came)
    near_v_on = pass_v(v_half, v_slot(side_a))
    stay, across, stay_on, across_on = [], [], [], []
    for p in range(2):
        w_own, w_other = w_slot(p, me_c), w_slot(p, side_c)
        stay.append(send_w(p, me_a, w_own, w_came))
        across.append(send_w(p, far_a, w_own, w_came))
        stay_on.append(pass_w(p, w_other, w_other))
        across_on.append(pass_w(p, w_half(p), w_other))

    def far(number, here, there):
        for b in others:
            there(number, b * SPLIT + far_a)
            here(number, b * SPLIT + me_a)

    for number in numbers:
        far(number, stay[0], across[0])
        near_v(number, far_c)
        across[0](number, far_c)
        send_w(0, side_far, w_half(0), w_side)(number, side_c)
        send_v(side_far, v_half, v_side)(number, side_c)
        send_w(0, side_a, w_slot(0, me_c), w_side)(number, side_c)
        send_v(side_a, v_own, v_side)(number, side_c)
    for number in numbers:
        send_w(1, side_far, w_half(1), w_side)(number, side_c)
        send_w(1, side_a, w_slot(1, me_c), w_side)(number, side_c)
    for number in numbers:
        start(
            lambda src: pltpu.make_async_copy(src, v_own(number), l_sem.at[0]),
            v_ref, v_tail, me_a, number,
        )
        start(
            lambda src: pltpu.make_async_copy(src, w_s.at[:, me_c, :, cols_of(number)], l_sem.at[1]),
            w_ref, w_tail, me_a, number,
        )

    for number in numbers:
        wait(w_s.at[0, pl.ds(0, 2), :, cols_of(number)], w_side.at[0, number])
        wait(v_s.at[pl.ds(0, 2), :, cols_of(number)], v_side.at[number])
        far(number, stay_on[0], across_on[0])
        near_v_on(number, far_c)
        across_on[0](number, far_c)

    @pl.when(inner)
    def _():
        for number in numbers:
            for b in others:
                across[1](number, b * SPLIT + far_a)

    for number in numbers[:early]:

        @pl.when(jnp.logical_not(inner))
        def _():
            far(number, stay[1], across[1])

        across[1](number, far_c)
    for number in numbers:
        wait(w_s.at[1, pl.ds(0, 2), :, cols_of(number)], w_side.at[1, number])

        @pl.when(inner)
        def _():
            for b in others:
                across_on[1](number, b * SPLIT + far_a)

        if number < early:

            @pl.when(jnp.logical_not(inner))
            def _():
                far(number, stay_on[1], across_on[1])

            across_on[1](number, far_c)

    @pl.when(inner)
    def _():
        for number in numbers:
            for b in others:
                stay[1](number, b * SPLIT + me_a)
                stay_on[1](number, b * SPLIT + me_a)

    def panel_of(p, cols):
        block = w_s[p, :, :, cols]
        if w_s.shape[2] % 16:
            block = block.astype(F32)
        return block.reshape(panel, block.shape[-1]).astype(BF16)

    def products(p, at, stop):
        cols = pl.ds(at, stop - at)
        v = v_s[:, :, cols].reshape(rows, stop - at)
        part[...] += lax.dot_general(v, panel_of(p, cols), NT, preferred_element_type=F32)

    def factor_of(p, sums):
        s_s[...] = lax.dot_general(
            sums, t_s[p], NT, precision=lax.Precision.HIGHEST, preferred_element_type=F32
        ).astype(BF16)

    def update(p, at, stop):
        @pl.loop(at // n_block, stop // n_block)
        def _(i):
            cols = pl.ds(pl.multiple_of(i * n_block, n_block), n_block)
            v = v_s[:, :, cols].reshape(rows, n_block).astype(F32)
            v = v - jnp.dot(s_s[...], panel_of(p, cols), preferred_element_type=F32)
            v_s[:, :, cols] = v.astype(BF16).reshape(SPLIT, rows // SPLIT, n_block)

    wait(v_s.at[0, :, pl.ds(0, site)], l_sem.at[0])
    wait(w_s.at[:, 0, :, pl.ds(0, site)], l_sem.at[1])
    for number in numbers:
        wait(v_s.at[pl.ds(0, 2), :, cols_of(number)], v_came.at[number])
        wait(w_s.at[0, pl.ds(0, n_col - 2), :, cols_of(number)], w_came.at[0, number])
        products(0, *sums_at[number])

    m_send[...] = part[...].reshape(m_send.shape)
    part[...] = jnp.zeros_like(part)
    for g, r, c in near_by:
        h = lax.rem(g, plane)
        remote(m_send.at[h], m_recv.at[me_h], m_sems.at[0], m_sems.at[1], r, c).start()
    m_recv[me_h] = m_send[me_h]
    wait(m_recv.at[pl.ds(0, plane - 1)], m_sems.at[1])
    z_send[...] = jnp.sum(m_recv[...], axis=0)
    remote(z_send, z_recv, m_sems.at[2], m_sems.at[3], me_r, far_c).start()
    for number in numbers[early:]:

        @pl.when(jnp.logical_not(inner))
        def _():
            far(number, stay[1], across[1])

        across[1](number, far_c)

        @pl.when(jnp.logical_not(inner))
        def _():
            far(number, stay_on[1], across_on[1])

        across_on[1](number, far_c)
    wait(z_recv, m_sems.at[3])
    m_all[me_h] = z_send[...] + z_recv[...]
    for _, r, c in near_by:
        remote(m_all.at[me_h], m_all.at[me_h], m_sems.at[4], m_sems.at[5], r, c).start()
    keep_t.wait()
    wait(m_all.at[pl.ds(0, plane - 1)], m_sems.at[5])
    factor_of(0, m_all[...].reshape(rows, panel))
    update(0, 0, width)

    for number in numbers:
        wait(w_s.at[1, pl.ds(0, n_col - 2), :, cols_of(number)], w_came.at[1, number])
        products(1, *sums_at[number])

    rs_send[...] = part[...].astype(BF16).reshape(rs_send.shape)
    for g, r, c in partners:
        remote(rs_send.at[g], rs_recv.at[me_g], r_send, r_recv, r, c).start()
    rs_recv[me_g] = rs_send[me_g]
    wait(rs_recv.at[pl.ds(0, group - 1)], r_recv)
    ag[me_g] = jnp.sum(rs_recv[...].astype(F32), axis=0).astype(BF16)
    for g, r, c in partners:
        remote(ag.at[me_g], ag.at[me_g], g_send, g_recv, r, c).start()
    wait(ag.at[pl.ds(0, group - 1)], g_recv)
    factor_of(1, ag[...].reshape(rows, panel).astype(F32))

    def rows_of(r):
        return pl.ds(pl.multiple_of(r * own, own), own)

    for j, (at, stop) in enumerate(out_blocks):
        update(1, at, stop)
        cols = pl.ds(at, min(stop, site) - at)
        for g, r, c in partners:
            remote(
                v_s.at[lax.div(g, n_row), rows_of(r), cols], stage.at[me_g, :, cols],
                o_send, o_recv.at[j], r, c,
            ).start()

    for j, (at, stop) in enumerate(out_blocks):
        size = min(stop, site) - at
        cols = pl.ds(at, size)
        stage[me_g, :, cols] = v_s[me_a, rows_of(me_r), cols]
        wait(stage.at[pl.ds(0, group - 1), :, cols], o_recv.at[j])
        for r in range(n_row):
            for a in range(SPLIT):
                size = min(at + size, columns - a * site) - at
                begin = r * columns + a * site + at
                if size > 0:
                    o_ref[:, begin:begin + size] = stage[a * n_row + r, :, at:at + size]
                size = min(stop, site) - at
    wait(v_s.at[:, :, pl.ds(0, site)], v_sent)
    wait(w_s.at[:, :, :, pl.ds(0, site)], w_sent)
    wait(m_recv.at[pl.ds(0, plane - 1)], m_sems.at[0])
    wait(z_send, m_sems.at[2])
    wait(m_all.at[pl.ds(0, plane - 1)], m_sems.at[4])
    wait(rs_recv.at[pl.ds(0, group - 1)], r_send)
    wait(ag.at[pl.ds(0, group - 1)], g_send)
    wait(stage.at[pl.ds(0, group - 1)], o_send)


def body(n_row, n_col, vectors, reflectors, panel_factor):
    own_rows, columns = vectors.shape
    part_rows, panel = reflectors.shape[1], panel_factor.shape[1]
    group, plane, rows = SPLIT * n_row, 2 * n_row, SPLIT * own_rows
    site = -(-columns // (SPLIT * LANES)) * LANES
    last = columns - (SPLIT - 1) * site
    main, rest = last // LANES * LANES, last % LANES
    n_block = 2 * LANES
    width = -(-site // n_block) * n_block
    step = -(-main // (4 * n_block)) * n_block
    cuts = list(range(0, main, step)) + [main]
    even = main // n_block * n_block
    pieces = tuple(zip(cuts[:-1], cuts[1:])) + ((main, site),)
    sums_at = tuple((s, min(e, even)) for s, e in pieces[:-1]) + ((even, width),)
    marks = [0, 2 * n_block]
    blocks = width // n_block
    marks += [n_block * (2 + (blocks - 2) * k // 6) for k in range(1, 7)]
    out_blocks = tuple(zip(marks[:-1], marks[1:]))
    edge = min(((SPLIT - 1) * site + main) // LANES, -(-columns // LANES) - 1)
    count = len(pieces)
    dma = pltpu.SemaphoreType.DMA
    plan = (site, main, rest, pieces, sums_at, out_blocks, n_block, 2)
    whole = pl.pallas_call(
        functools.partial(kernel, n_row, n_col, columns, plan),
        grid=(1,),
        out_shape=jax.ShapeDtypeStruct((own_rows // n_row, n_row * columns), BF16),
        in_specs=[
            pl.BlockSpec(memory_space=pl.ANY),
            pl.BlockSpec(memory_space=pl.ANY),
            pl.BlockSpec((own_rows, LANES), lambda i: (0, edge)),
            pl.BlockSpec((2, part_rows, LANES), lambda i: (0, 0, edge)),
            pl.BlockSpec(memory_space=pltpu.HBM),
        ],
        out_specs=pl.BlockSpec(memory_space=pltpu.VMEM),
        scratch_shapes=[
            pltpu.VMEM((SPLIT, own_rows, width), BF16),
            pltpu.VMEM((2, n_col, part_rows, width), BF16),
            pltpu.VMEM((own_rows, site), BF16),
            pltpu.VMEM((2, part_rows, site), BF16),
            pltpu.VMEM((own_rows, site - main), BF16),
            pltpu.VMEM((2, part_rows, site - main), BF16),
            pltpu.VMEM(panel_factor.shape, F32),
            pltpu.VMEM((rows, panel), F32),
            pltpu.VMEM((rows, panel), BF16),
            pltpu.VMEM((group, own_rows // n_row, site), BF16),
            pltpu.VMEM((plane, rows // plane, panel), F32),
            pltpu.VMEM((plane, rows // plane, panel), F32),
            pltpu.VMEM((rows // plane, panel), F32),
            pltpu.VMEM((rows // plane, panel), F32),
            pltpu.VMEM((plane, rows // plane, panel), F32),
            pltpu.VMEM((group, rows // group, panel), BF16),
            pltpu.VMEM((group, rows // group, panel), BF16),
            pltpu.VMEM((group, rows // group, panel), BF16),
            dma, dma, dma((count,)), dma((2, count)), dma((count,)), dma((2, count)), dma((2,)), dma,
            dma((6,)), dma, dma, dma, dma, dma, dma((len(out_blocks),)),
        ],
        compiler_params=pltpu.CompilerParams(
            has_side_effects=True, collective_id=0, vmem_limit_bytes=48 * 1024 * 1024
        ),
        name="panels",
    )(
        vectors, reflectors, vectors, reflectors,
        pltpu.with_memory_space_constraint(panel_factor, pltpu.HBM),
    )
    return whole[None]


def solution(mesh):
    placed = (P("pcol", "prow"), P(None, "pcol", "prow"), P())
    return jax.shard_map(
        functools.partial(body, mesh.shape["prow"], mesh.shape["pcol"]),
        mesh=mesh, in_specs=placed, out_specs=P("pcol", "prow", None), check_vma=False,
    )
```

time: 237 us -> 231 us (0.975)
  Pallas kernels: 234 us -> 229 us
    pallas_call x1, Pallas kernels: 234 us -> 229 us  [body(): pl.pallas_call(functools.partial(kernel, n_row, n_col, columns, plan), gr...]
where the time goes in v3:
time: 231 us
  Pallas kernels  229 us (99%)
    pallas_call x1, Pallas kernels, body(): pl.pallas_call(functools.partial(kernel, n_row, n_col, columns, plan), gr...  229 us

profile of v3, /device:TPU:0, one launch (start us, length us, event | category | flops | bytes accessed | tf_op | source)
XLA Modules:
  0.0 230.6 jit_solution(9775806167207629034)
XLA Ops:
  0.0 228.7 %panels.1 = bf16[16,120064]{1,0:T(8,128)(2,1)S(1)} custom-call(bf16[64,30016]{1,0:T(8,128)(2,1)} %vt_ref.1, bf16[2,32,30016]{2,1,0:T(8,128)(2,1)} %wt_ref.1, bf16[64,30016]{1,0:T(8,128)(2,1)} %vt_ref.1, bf16[2,32,30016]{2,1,0:T(8,128)(2,1)} %wt_ref.1, f32[2,256,256]{2,1,0:T(8,128)} %t_ref.1), custom_call_target="tpu_custom_call" | custom-call | tf_op jit(solution)/shard_map/panels/pallas_call | solution.py:363
  228.7 1.9 copy.5

commit v4 on v3

--- a/solution.py
+++ b/solution.py
@@ -32,10 +32,10 @@
     v_ref, w_ref, vt_ref, wt_ref, t_ref, o_ref,
     v_s, w_s, v_mid, w_mid, v_tail, w_tail, t_s, part, s_s, stage,
     m_send, m_recv, z_send, z_recv, m_all, rs_send, rs_recv, ag,
-    v_sent, w_sent, v_came, w_came, v_side, w_side, l_sem, t_sem,
-    m_sems, r_send, r_recv, g_send, g_recv, o_send, o_recv,
+    v_sent, w_sent, v_came, w_came, v_side, w_side, l_sem, t_sem, lend_sent, lend_came,
+    m_sems, r_send, r_recv, g_send, g_recv, o_send, o_recv, entered,
 ):
-    site, main, rest, pieces, sums_at, out_blocks, n_block, early = plan
+    site, main, rest, pieces, sums_at, out_blocks, n_block, early, lent = plan
     me_r, me_c = lax.axis_index("prow"), lax.axis_index("pcol")
     me_a, me_b = lax.rem(me_c, SPLIT), lax.div(me_c, SPLIT)
     me_x, me_e = lax.rem(me_a, 2), lax.div(me_a, 2)
@@ -61,17 +61,37 @@
         a, r = flipped(me_a, mask // n_row), flipped(me_r, mask % n_row)
         return a * n_row + r, r, me_b * SPLIT + a
 
-    partners = [partner(mask) for mask in sorted(range(1, group), key=turns)]
-    near_by = [partner(mask) for mask in sorted(range(1, plane), key=turns)]
-
+    masks = sorted(range(1, group), key=turns)
+    partners = [partner(mask) for mask in masks]
+    near_by = [partner(mask) for mask in masks if mask < plane]
+
+    def earlier(mask):
+        top = 1
+        while 2 * top <= mask:
+            top *= 2
+        if top >= n_row:
+            return lax.rem(lax.div(me_a, top // n_row), 2) == 1
+        return lax.rem(lax.div(me_r, top), 2) == (0 if top == 1 else 1)
+
+    met = [
+        (earlier(mask), r, c, {n_row: 0, 2 * n_row: 1}.get(mask, 3))
+        for mask, (_, r, c) in zip(masks, partners)
+    ]
+    met += [(b < me_b, me_r, b * SPLIT + a, 2) for b in others for a in (me_a, far_a)]
+    ahead = [met[masks.index(n_row)][0], met[masks.index(2 * n_row)][0]]
     barrier = pltpu.get_barrier_semaphore()
-    for _, r, c in partners:
-        pl.semaphore_signal(barrier, device_id={"prow": r, "pcol": c}, device_id_type=MESH)
-    for b in others:
-        for a in (me_a, far_a):
-            pl.semaphore_signal(
-                barrier, device_id={"prow": me_r, "pcol": b * SPLIT + a}, device_id_type=MESH
-            )
+    for early_one, r, c, _ in met:
+
+        @pl.when(jnp.logical_not(early_one))
+        def _():
+            pl.semaphore_signal(barrier, device_id={"prow": r, "pcol": c}, device_id_type=MESH)
+
+    def count_of(kind, early_ones):
+        flags = [m[0] if early_ones else jnp.logical_not(m[0]) for m in met if kind in (m[3], None)]
+        return sum(flag.astype(jnp.int32) for flag in flags)
+
+    def wait_for(sem, count):
+        pl.when(count > 0)(lambda: pl.semaphore_wait(sem, count))
 
     def remote(src, dst, send, recv, r, c):
         return pltpu.make_async_remote_copy(
@@ -107,6 +127,9 @@
     def w_half(p):
         return lambda number: w_mid.at[p, :, cols_of(number)]
 
+    def sent_of(p, number):
+        return 0 if p else 1 if number < lent else 2
+
     def send_v(q, dst, come):
         def start_copy(number, c):
             start(
@@ -118,7 +141,7 @@
     def send_w(p, q, dst, come):
         def start_copy(number, c):
             start(
-                lambda src: remote(src, dst(number), w_sent, come.at[p, number], me_r, c),
+                lambda src: remote(src, dst(number), w_sent.at[sent_of(p, number)], come.at[p, number], me_r, c),
                 w_ref.at[p], w_tail.at[p], q, number,
             )
         return start_copy
@@ -130,7 +153,9 @@
 
     def pass_w(p, src, dst):
         def start_copy(number, c):
-            remote(src(number), dst(number), w_sent, w_came.at[p, number], me_r, c).start()
+            remote(
+                src(number), dst(number), w_sent.at[sent_of(p, number)], w_came.at[p, number], me_r, c
+            ).start()
         return start_copy
 
     keep_t = pltpu.make_async_copy(t_ref, t_s, t_sem)
@@ -145,7 +170,14 @@
         v_s[:, :, site:] = jnp.zeros((SPLIT, v_s.shape[1], width - site), BF16)
         w_s[:, :, :, site:] = jnp.zeros((2, n_col, w_s.shape[2], width - site), BF16)
     part[...] = jnp.zeros_like(part)
-    pl.semaphore_wait(barrier, len(partners) + 2 * len(others))
+    wait_for(barrier, count_of(None, True))
+    for early_one, r, c, kind in met:
+
+        @pl.when(early_one)
+        def _():
+            pl.semaphore_signal(
+                entered.at[kind], device_id={"prow": r, "pcol": c}, device_id_type=MESH
+            )
 
     v_own = v_slot(me_a)
     near_v = send_v(far_a, v_own, v_came)
@@ -163,10 +195,41 @@
             there(number, b * SPLIT + far_a)
             here(number, b * SPLIT + me_a)
 
-    for number in numbers:
-        far(number, stay[0], across[0])
+    to_lender = send_w(0, far_a, w_slot(0, me_c), lend_came)
+
+    def near(number):
         near_v(number, far_c)
-        across[0](number, far_c)
+        if number < lent:
+            pl.when(inner)(functools.partial(across[0], number, far_c))
+            pl.when(jnp.logical_not(inner))(functools.partial(to_lender, number, far_c))
+        else:
+            across[0](number, far_c)
+
+    def over(number, c):
+        if number < lent:
+
+            @pl.when(inner)
+            def _():
+                start(
+                    lambda src: remote(
+                        src, w_slot(0, me_c)(number), lend_sent, w_came.at[0, number], me_r, c
+                    ),
+                    w_ref.at[0], w_tail.at[0], far_a, number,
+                )
+        else:
+            across[0](number, c)
+
+    for number in numbers:
+        for b in others:
+
+            @pl.when(b < me_b)
+            def _():
+                over(number, b * SPLIT + far_a)
+                stay[0](number, b * SPLIT + me_a)
+
+        pl.when(ahead[1])(functools.partial(near, number))
+    wait_for(entered.at[0], count_of(0, False))
+    for number in numbers:
         send_w(0, side_far, w_half(0), w_side)(number, side_c)
         send_v(side_far, v_half, v_side)(number, side_c)
         send_w(0, side_a, w_slot(0, me_c), w_side)(number, side_c)
@@ -174,6 +237,25 @@
     for number in numbers:
         send_w(1, side_far, w_half(1), w_side)(number, side_c)
         send_w(1, side_a, w_slot(1, me_c), w_side)(number, side_c)
+    wait_for(entered.at[1], count_of(1, False))
+    pl.when(jnp.logical_not(ahead[1]))(functools.partial(near, 0))
+    wait_for(entered.at[2], count_of(2, False))
+    for number in numbers:
+        for b in others:
+
+            @pl.when(b > me_b)
+            def _():
+                over(number, b * SPLIT + far_a)
+                stay[0](number, b * SPLIT + me_a)
+
+        if number:
+            pl.when(jnp.logical_not(ahead[1]))(functools.partial(near, number))
+    @pl.when(inner)
+    def _():
+        for number in numbers:
+            for b in others:
+                across[1](number, b * SPLIT + far_a)
+
     for number in numbers:
         start(
             lambda src: pltpu.make_async_copy(src, v_own(number), l_sem.at[0]),
@@ -191,11 +273,17 @@
         near_v_on(number, far_c)
         across_on[0](number, far_c)
 
-    @pl.when(inner)
-    def _():
-        for number in numbers:
-            for b in others:
-                across[1](number, b * SPLIT + far_a)
+    if lent:
+
+        @pl.when(inner)
+        def _():
+            for number in numbers[:lent]:
+                lend = w_slot(0, far_c)(number)
+                wait(lend, lend_came.at[0, number])
+                for b in others:
+                    remote(
+                        lend, lend, lend_sent, w_came.at[0, number], me_r, b * SPLIT + me_a
+                    ).start()
 
     for number in numbers[:early]:
 
@@ -239,7 +327,7 @@
         part[...] += lax.dot_general(v, panel_of(p, cols), NT, preferred_element_type=F32)
 
     def factor_of(p, sums):
-        s_s[...] = lax.dot_general(
+        return lax.dot_general(
             sums, t_s[p], NT, precision=lax.Precision.HIGHEST, preferred_element_type=F32
         ).astype(BF16)
 
@@ -255,10 +343,17 @@
     wait(w_s.at[:, 0, :, pl.ds(0, site)], l_sem.at[1])
     for number in numbers:
         wait(v_s.at[pl.ds(0, 2), :, cols_of(number)], v_came.at[number])
-        wait(w_s.at[0, pl.ds(0, n_col - 2), :, cols_of(number)], w_came.at[0, number])
+        if number < lent:
+            for own_role, slots in ((inner, n_col - 3), (jnp.logical_not(inner), n_col - 2)):
+                pl.when(own_role)(functools.partial(
+                    wait, w_s.at[0, pl.ds(0, slots), :, cols_of(number)], w_came.at[0, number]
+                ))
+        else:
+            wait(w_s.at[0, pl.ds(0, n_col - 2), :, cols_of(number)], w_came.at[0, number])
         products(0, *sums_at[number])
 
     m_send[...] = part[...].reshape(m_send.shape)
+    wait_for(entered.at[3], count_of(3, False))
     part[...] = jnp.zeros_like(part)
     for g, r, c in near_by:
         h = lax.rem(g, plane)
@@ -286,7 +381,7 @@
         remote(m_all.at[me_h], m_all.at[me_h], m_sems.at[4], m_sems.at[5], r, c).start()
     keep_t.wait()
     wait(m_all.at[pl.ds(0, plane - 1)], m_sems.at[5])
-    factor_of(0, m_all[...].reshape(rows, panel))
+    s_s[...] = factor_of(0, m_all[...].reshape(rows, panel))
     update(0, 0, width)
 
     for number in numbers:
@@ -298,11 +393,11 @@
         remote(rs_send.at[g], rs_recv.at[me_g], r_send, r_recv, r, c).start()
     rs_recv[me_g] = rs_send[me_g]
     wait(rs_recv.at[pl.ds(0, group - 1)], r_recv)
-    ag[me_g] = jnp.sum(rs_recv[...].astype(F32), axis=0).astype(BF16)
+    ag[me_g] = factor_of(1, jnp.sum(rs_recv[...].astype(F32), axis=0))
     for g, r, c in partners:
         remote(ag.at[me_g], ag.at[me_g], g_send, g_recv, r, c).start()
     wait(ag.at[pl.ds(0, group - 1)], g_recv)
-    factor_of(1, ag[...].reshape(rows, panel).astype(F32))
+    s_s[...] = ag[...].reshape(rows, panel)
 
     def rows_of(r):
         return pl.ds(pl.multiple_of(r * own, own), own)
@@ -329,7 +424,16 @@
                     o_ref[:, begin:begin + size] = stage[a * n_row + r, :, at:at + size]
                 size = min(stop, site) - at
     wait(v_s.at[:, :, pl.ds(0, site)], v_sent)
-    wait(w_s.at[:, :, :, pl.ds(0, site)], w_sent)
+    cut = pieces[lent][0]
+    wait(w_s.at[1, :, :, pl.ds(0, site)], w_sent.at[0])
+    if lent:
+        wait(w_s.at[0, pl.ds(0, n_col - len(others)), :, pl.ds(0, cut)], w_sent.at[1])
+
+        @pl.when(inner)
+        def _():
+            wait(w_s.at[0, pl.ds(0, 2 * len(others)), :, pl.ds(0, cut)], lend_sent)
+
+    wait(w_s.at[0, :, :, pl.ds(cut, site - cut)], w_sent.at[2])
     wait(m_recv.at[pl.ds(0, plane - 1)], m_sems.at[0])
     wait(z_send, m_sems.at[2])
     wait(m_all.at[pl.ds(0, plane - 1)], m_sems.at[4])
@@ -359,7 +463,7 @@
     edge = min(((SPLIT - 1) * site + main) // LANES, -(-columns // LANES) - 1)
     count = len(pieces)
     dma = pltpu.SemaphoreType.DMA
-    plan = (site, main, rest, pieces, sums_at, out_blocks, n_block, 2)
+    plan = (site, main, rest, pieces, sums_at, out_blocks, n_block, 2, 2)
     whole = pl.pallas_call(
         functools.partial(kernel, n_row, n_col, columns, plan),
         grid=(1,),
@@ -391,8 +495,10 @@
             pltpu.VMEM((group, rows // group, panel), BF16),
             pltpu.VMEM((group, rows // group, panel), BF16),
             pltpu.VMEM((group, rows // group, panel), BF16),
-            dma, dma, dma((count,)), dma((2, count)), dma((count,)), dma((2, count)), dma((2,)), dma,
+            dma, dma((3,)), dma((count,)), dma((2, count)), dma((count,)), dma((2, count)), dma((2,)), dma,
+            dma, dma((1, count)),
             dma((6,)), dma, dma, dma, dma, dma, dma((len(out_blocks),)),
+            pltpu.SemaphoreType.REGULAR((4,)),
         ],
         compiler_params=pltpu.CompilerParams(
             has_side_effects=True, collective_id=0, vmem_limit_bytes=48 * 1024 * 1024

time: 231 us -> 229 us (level)
  no operation moved by 1% of the time
where the time goes in v4:
time: 229 us
  Pallas kernels  227 us (99%)
    pallas_call x1, Pallas kernels, body(): pl.pallas_call(functools.partial(kernel, n_row, n_col, columns, plan), gr...  227 us

profile of v4, /device:TPU:0, one launch (start us, length us, event | category | flops | bytes accessed | tf_op | source)
XLA Modules:
  0.0 228.6 jit_solution(6374884847448976578)
XLA Ops:
  0.0 226.7 %panels.1 = bf16[16,120064]{1,0:T(8,128)(2,1)S(1)} custom-call(bf16[64,30016]{1,0:T(8,128)(2,1)} %vt_ref.1, bf16[2,32,30016]{2,1,0:T(8,128)(2,1)} %wt_ref.1, bf16[64,30016]{1,0:T(8,128)(2,1)} %vt_ref.1, bf16[2,32,30016]{2,1,0:T(8,128)(2,1)} %wt_ref.1, f32[2,256,256]{2,1,0:T(8,128)} %t_ref.1), custom_call_target="tpu_custom_call" | custom-call | tf_op jit(solution)/shard_map/panels/pallas_call | solution.py:467
  226.7 1.9 copy.5

commit v5 on v4

--- a/solution.py
+++ b/solution.py
@@ -33,7 +33,7 @@
     v_s, w_s, v_mid, w_mid, v_tail, w_tail, t_s, part, s_s, stage,
     m_send, m_recv, z_send, z_recv, m_all, rs_send, rs_recv, ag,
     v_sent, w_sent, v_came, w_came, v_side, w_side, l_sem, t_sem, lend_sent, lend_came,
-    m_sems, r_send, r_recv, g_send, g_recv, o_send, o_recv, entered,
+    m_sems, r_send, r_recv, g_send, g_recv, o_send, o_recv, entered, told,
 ):
     site, main, rest, pieces, sums_at, out_blocks, n_block, early, lent = plan
     me_r, me_c = lax.axis_index("prow"), lax.axis_index("pcol")
@@ -73,12 +73,13 @@
             return lax.rem(lax.div(me_a, top // n_row), 2) == 1
         return lax.rem(lax.div(me_r, top), 2) == (0 if top == 1 else 1)
 
+    steps = [1 << bit for bit in range(group.bit_length() - 1)]
     met = [
-        (earlier(mask), r, c, {n_row: 0, 2 * n_row: 1}.get(mask, 3))
-        for mask, (_, r, c) in zip(masks, partners)
+        (earlier(mask), *partner(mask)[1:], {n_row: 0, 2 * n_row: 1}.get(mask, 3))
+        for mask in steps
     ]
     met += [(b < me_b, me_r, b * SPLIT + a, 2) for b in others for a in (me_a, far_a)]
-    ahead = [met[masks.index(n_row)][0], met[masks.index(2 * n_row)][0]]
+    ahead = [earlier(n_row), earlier(2 * n_row)]
     barrier = pltpu.get_barrier_semaphore()
     for early_one, r, c, _ in met:
 
@@ -315,6 +316,12 @@
                 stay[1](number, b * SPLIT + me_a)
                 stay_on[1](number, b * SPLIT + me_a)
 
+    wait_for(entered.at[3], count_of(3, False))
+    for k, mask in enumerate(steps):
+        _, r, c = partner(mask)
+        pl.semaphore_signal(told.at[k], device_id={"prow": r, "pcol": c}, device_id_type=MESH)
+        pl.semaphore_wait(told.at[k], 1)
+
     def panel_of(p, cols):
         block = w_s[p, :, :, cols]
         if w_s.shape[2] % 16:
@@ -353,7 +360,6 @@
         products(0, *sums_at[number])
 
     m_send[...] = part[...].reshape(m_send.shape)
-    wait_for(entered.at[3], count_of(3, False))
     part[...] = jnp.zeros_like(part)
     for g, r, c in near_by:
         h = lax.rem(g, plane)
@@ -499,6 +505,7 @@
             dma, dma((1, count)),
             dma((6,)), dma, dma, dma, dma, dma, dma((len(out_blocks),)),
             pltpu.SemaphoreType.REGULAR((4,)),
+            pltpu.SemaphoreType.REGULAR((group.bit_length() - 1,)),
         ],
         compiler_params=pltpu.CompilerParams(
             has_side_effects=True, collective_id=0, vmem_limit_bytes=48 * 1024 * 1024

time: 229 us -> 228 us (level)
  no operation moved by 1% of the time
where the time goes in v5:
time: 228 us
  Pallas kernels  226 us (99%)
    pallas_call x1, Pallas kernels, body(): pl.pallas_call(functools.partial(kernel, n_row, n_col, columns, plan), gr...  226 us

profile of v5, /device:TPU:0, one launch (start us, length us, event | category | flops | bytes accessed | tf_op | source)
XLA Modules:
  0.0 227.5 jit_solution(13819698007020536312)
XLA Ops:
  0.0 225.6 %panels.1 = bf16[16,120064]{1,0:T(8,128)(2,1)S(1)} custom-call(bf16[64,30016]{1,0:T(8,128)(2,1)} %vt_ref.1, bf16[2,32,30016]{2,1,0:T(8,128)(2,1)} %wt_ref.1, bf16[64,30016]{1,0:T(8,128)(2,1)} %vt_ref.1, bf16[2,32,30016]{2,1,0:T(8,128)(2,1)} %wt_ref.1, f32[2,256,256]{2,1,0:T(8,128)} %t_ref.1), custom_call_target="tpu_custom_call" | custom-call | tf_op jit(solution)/shard_map/panels/pallas_call | solution.py:473
  225.6 1.9 copy.5

commit v6 on v5

--- a/solution.py
+++ b/solution.py
@@ -29,8 +29,8 @@
 
 def kernel(
     n_row, n_col, columns, plan,
-    v_ref, w_ref, vt_ref, wt_ref, t_ref, o_ref,
-    v_s, w_s, v_mid, w_mid, v_tail, w_tail, t_s, part, s_s, stage,
+    v_ref, w_ref, t_ref, o_ref,
+    v_s, w_s, v_mid, w_mid, v_tail, w_tail, v_all, w_all, t_s, part, s_s, stage,
     m_send, m_recv, z_send, z_recv, m_all, rs_send, rs_recv, ag,
     v_sent, w_sent, v_came, w_came, v_side, w_side, l_sem, t_sem, lend_sent, lend_came,
     m_sems, r_send, r_recv, g_send, g_recv, o_send, o_recv, entered, told,
@@ -159,13 +159,14 @@
             ).start()
         return start_copy
 
-    keep_t = pltpu.make_async_copy(t_ref, t_s, t_sem)
+    keep_t = pltpu.make_async_copy(t_ref, t_s, t_sem.at[0])
     keep_t.start()
-    v_tail[...] = jnp.zeros_like(v_tail)
-    w_tail[...] = jnp.zeros_like(w_tail)
-    if rest:
-        v_tail[:, :rest] = vt_ref[:, :rest]
-        w_tail[:, :, :rest] = wt_ref[:, :, :rest]
+    whole = [
+        pltpu.make_async_copy(v_ref, v_all, t_sem.at[1]),
+        pltpu.make_async_copy(w_ref, w_all, t_sem.at[2]),
+    ]
+    for copy in whole:
+        copy.start()
     width = v_s.shape[2]
     if width > site:
         v_s[:, :, site:] = jnp.zeros((SPLIT, v_s.shape[1], width - site), BF16)
@@ -220,7 +221,7 @@
         else:
             across[0](number, c)
 
-    for number in numbers:
+    def to_earlier(number):
         for b in others:
 
             @pl.when(b < me_b)
@@ -229,28 +230,48 @@
                 stay[0](number, b * SPLIT + me_a)
 
         pl.when(ahead[1])(functools.partial(near, number))
-    wait_for(entered.at[0], count_of(0, False))
-    for number in numbers:
+
+    def to_later(number):
+        for b in others:
+
+            @pl.when(b > me_b)
+            def _():
+                over(number, b * SPLIT + far_a)
+                stay[0](number, b * SPLIT + me_a)
+
+        if number:
+            pl.when(jnp.logical_not(ahead[1]))(functools.partial(near, number))
+
+    def to_side(number):
         send_w(0, side_far, w_half(0), w_side)(number, side_c)
         send_v(side_far, v_half, v_side)(number, side_c)
         send_w(0, side_a, w_slot(0, me_c), w_side)(number, side_c)
         send_v(side_a, v_own, v_side)(number, side_c)
+
+    for number in numbers[:-1]:
+        to_earlier(number)
+    wait_for(entered.at[0], count_of(0, False))
+    for number in numbers[:-1]:
+        to_side(number)
+    wait_for(entered.at[1], count_of(1, False))
+    pl.when(jnp.logical_not(ahead[1]))(functools.partial(near, 0))
+    wait_for(entered.at[2], count_of(2, False))
+    for number in numbers[:-1]:
+        to_later(number)
+    v_tail[...] = jnp.zeros_like(v_tail)
+    w_tail[...] = jnp.zeros_like(w_tail)
+    for copy in whole:
+        copy.wait()
+    if rest:
+        edge = (SPLIT - 1) * site + main
+        v_tail[:, :rest] = v_all[:, edge:edge + rest]
+        w_tail[:, :, :rest] = w_all[:, :, edge:edge + rest]
+    for send_last in (to_earlier, to_side, to_later):
+        send_last(numbers[-1])
     for number in numbers:
         send_w(1, side_far, w_half(1), w_side)(number, side_c)
         send_w(1, side_a, w_slot(1, me_c), w_side)(number, side_c)
-    wait_for(entered.at[1], count_of(1, False))
-    pl.when(jnp.logical_not(ahead[1]))(functools.partial(near, 0))
-    wait_for(entered.at[2], count_of(2, False))
-    for number in numbers:
-        for b in others:
-
-            @pl.when(b > me_b)
-            def _():
-                over(number, b * SPLIT + far_a)
-                stay[0](number, b * SPLIT + me_a)
-
-        if number:
-            pl.when(jnp.logical_not(ahead[1]))(functools.partial(near, number))
+
     @pl.when(inner)
     def _():
         for number in numbers:
@@ -466,19 +487,15 @@
     blocks = width // n_block
     marks += [n_block * (2 + (blocks - 2) * k // 6) for k in range(1, 7)]
     out_blocks = tuple(zip(marks[:-1], marks[1:]))
-    edge = min(((SPLIT - 1) * site + main) // LANES, -(-columns // LANES) - 1)
     count = len(pieces)
     dma = pltpu.SemaphoreType.DMA
     plan = (site, main, rest, pieces, sums_at, out_blocks, n_block, 2, 2)
     whole = pl.pallas_call(
         functools.partial(kernel, n_row, n_col, columns, plan),
-        grid=(1,),
         out_shape=jax.ShapeDtypeStruct((own_rows // n_row, n_row * columns), BF16),
         in_specs=[
             pl.BlockSpec(memory_space=pl.ANY),
             pl.BlockSpec(memory_space=pl.ANY),
-            pl.BlockSpec((own_rows, LANES), lambda i: (0, edge)),
-            pl.BlockSpec((2, part_rows, LANES), lambda i: (0, 0, edge)),
             pl.BlockSpec(memory_space=pltpu.HBM),
         ],
         out_specs=pl.BlockSpec(memory_space=pltpu.VMEM),
@@ -489,6 +506,8 @@
             pltpu.VMEM((2, part_rows, site), BF16),
             pltpu.VMEM((own_rows, site - main), BF16),
             pltpu.VMEM((2, part_rows, site - main), BF16),
+            pltpu.VMEM(vectors.shape, BF16),
+            pltpu.VMEM(reflectors.shape, BF16),
             pltpu.VMEM(panel_factor.shape, F32),
             pltpu.VMEM((rows, panel), F32),
             pltpu.VMEM((rows, panel), BF16),
@@ -501,7 +520,7 @@
             pltpu.VMEM((group, rows // group, panel), BF16),
             pltpu.VMEM((group, rows // group, panel), BF16),
             pltpu.VMEM((group, rows // group, panel), BF16),
-            dma, dma((3,)), dma((count,)), dma((2, count)), dma((count,)), dma((2, count)), dma((2,)), dma,
+            dma, dma((3,)), dma((count,)), dma((2, count)), dma((count,)), dma((2, count)), dma((2,)), dma((3,)),
             dma, dma((1, count)),
             dma((6,)), dma, dma, dma, dma, dma, dma((len(out_blocks),)),
             pltpu.SemaphoreType.REGULAR((4,)),
@@ -512,7 +531,7 @@
         ),
         name="panels",
     )(
-        vectors, reflectors, vectors, reflectors,
+        vectors, reflectors,
         pltpu.with_memory_space_constraint(panel_factor, pltpu.HBM),
     )
     return whole[None]

time: 228 us -> 227 us (level)
  no operation moved by 1% of the time
where the time goes in v6:
time: 227 us
  Pallas kernels  225 us (99%)
    pallas_call x1, Pallas kernels, body(): pl.pallas_call(functools.partial(kernel, n_row, n_col, columns, plan), ou...  225 us

profile of v6, /device:TPU:0, one launch (start us, length us, event | category | flops | bytes accessed | tf_op | source)
XLA Modules:
  0.0 226.8 jit_solution(1909116650895601954)
XLA Ops:
  0.0 224.9 %panels.1 = bf16[16,120064]{1,0:T(8,128)(2,1)S(1)} custom-call(bf16[64,30016]{1,0:T(8,128)(2,1)} %v_ref.1, bf16[2,32,30016]{2,1,0:T(8,128)(2,1)} %w_ref.1, f32[2,256,256]{2,1,0:T(8,128)} %t_ref.1), custom_call_target="tpu_custom_call" | custom-call | tf_op jit(solution)/shard_map/panels/pallas_call | solution.py:493
  224.9 1.9 copy.5

commit v7 on v6

--- a/solution.py
+++ b/solution.py
@@ -78,7 +78,8 @@
         (earlier(mask), *partner(mask)[1:], {n_row: 0, 2 * n_row: 1}.get(mask, 3))
         for mask in steps
     ]
-    met += [(b < me_b, me_r, b * SPLIT + a, 2) for b in others for a in (me_a, far_a)]
+    met += [(b < me_b, me_r, b * SPLIT + me_a, 2) for b in others]
+    met += [(b < me_b, me_r, b * SPLIT + far_a, 4) for b in others]
     ahead = [earlier(n_row), earlier(2 * n_row)]
     barrier = pltpu.get_barrier_semaphore()
     for early_one, r, c, _ in met:
@@ -236,7 +237,12 @@
 
             @pl.when(b > me_b)
             def _():
-                over(number, b * SPLIT + far_a)
+                if number:
+                    over(number, b * SPLIT + far_a)
+                else:
+                    pl.when(jnp.logical_not(inner))(
+                        functools.partial(over, 0, b * SPLIT + far_a)
+                    )
                 stay[0](number, b * SPLIT + me_a)
 
         if number:
@@ -255,6 +261,9 @@
         to_side(number)
     wait_for(entered.at[1], count_of(1, False))
     pl.when(jnp.logical_not(ahead[1]))(functools.partial(near, 0))
+    wait_for(entered.at[4], count_of(4, False))
+    for b in others:
+        pl.when(inner & (b > me_b))(functools.partial(over, 0, b * SPLIT + far_a))
     wait_for(entered.at[2], count_of(2, False))
     for number in numbers[:-1]:
         to_later(number)
@@ -317,10 +326,12 @@
     for number in numbers:
         wait(w_s.at[1, pl.ds(0, 2), :, cols_of(number)], w_side.at[1, number])
 
-        @pl.when(inner)
-        def _():
-            for b in others:
-                across_on[1](number, b * SPLIT + far_a)
+        if number < 3:
+
+            @pl.when(inner)
+            def _():
+                for b in others:
+                    across_on[1](number, b * SPLIT + far_a)
 
         if number < early:
 
@@ -336,6 +347,9 @@
             for b in others:
                 stay[1](number, b * SPLIT + me_a)
                 stay_on[1](number, b * SPLIT + me_a)
+        for number in numbers[3:]:
+            for b in others:
+                across_on[1](number, b * SPLIT + far_a)
 
     wait_for(entered.at[3], count_of(3, False))
     for k, mask in enumerate(steps):
@@ -523,7 +537,7 @@
             dma, dma((3,)), dma((count,)), dma((2, count)), dma((count,)), dma((2, count)), dma((2,)), dma((3,)),
             dma, dma((1, count)),
             dma((6,)), dma, dma, dma, dma, dma, dma((len(out_blocks),)),
-            pltpu.SemaphoreType.REGULAR((4,)),
+            pltpu.SemaphoreType.REGULAR((5,)),
             pltpu.SemaphoreType.REGULAR((group.bit_length() - 1,)),
         ],
         compiler_params=pltpu.CompilerParams(

time: 227 us -> 227 us (level)
  no operation moved by 1% of the time
where the time goes in v7:
time: 227 us
  Pallas kernels  225 us (99%)
    pallas_call x1, Pallas kernels, body(): pl.pallas_call(functools.partial(kernel, n_row, n_col, columns, plan), ou...  225 us

profile of v7, /device:TPU:0, one launch (start us, length us, event | category | flops | bytes accessed | tf_op | source)
XLA Modules:
  0.0 226.7 jit_solution(12284588199079162042)
XLA Ops:
  0.0 224.8 %panels.1 = bf16[16,120064]{1,0:T(8,128)(2,1)S(1)} custom-call(bf16[64,30016]{1,0:T(8,128)(2,1)} %v_ref.1, bf16[2,32,30016]{2,1,0:T(8,128)(2,1)} %w_ref.1, f32[2,256,256]{2,1,0:T(8,128)} %t_ref.1), custom_call_target="tpu_custom_call" | custom-call | tf_op jit(solution)/shard_map/panels/pallas_call | solution.py:507
  224.8 1.9 copy.5

commit v8 on v6

--- a/solution.py
+++ b/solution.py
@@ -483,9 +483,9 @@
     even = main // n_block * n_block
     pieces = tuple(zip(cuts[:-1], cuts[1:])) + ((main, site),)
     sums_at = tuple((s, min(e, even)) for s, e in pieces[:-1]) + ((even, width),)
-    marks = [0, 2 * n_block]
+    marks = [0, n_block]
     blocks = width // n_block
-    marks += [n_block * (2 + (blocks - 2) * k // 6) for k in range(1, 7)]
+    marks += [n_block * (1 + (blocks - 1) * k // 6) for k in range(1, 7)]
     out_blocks = tuple(zip(marks[:-1], marks[1:]))
     count = len(pieces)
     dma = pltpu.SemaphoreType.DMA

time: 227 us -> 227 us (level)
  no operation moved by 1% of the time
where the time goes in v8:
time: 227 us
  Pallas kernels  225 us (99%)
    pallas_call x1, Pallas kernels, body(): pl.pallas_call(functools.partial(kernel, n_row, n_col, columns, plan), ou...  225 us

profile of v8, /device:TPU:0, one launch (start us, length us, event | category | flops | bytes accessed | tf_op | source)
XLA Modules:
  0.0 226.7 jit_solution(16427107201733021883)
XLA Ops:
  0.0 224.8 %panels.1 = bf16[16,120064]{1,0:T(8,128)(2,1)S(1)} custom-call(bf16[64,30016]{1,0:T(8,128)(2,1)} %v_ref.1, bf16[2,32,30016]{2,1,0:T(8,128)(2,1)} %w_ref.1, f32[2,256,256]{2,1,0:T(8,128)} %t_ref.1), custom_call_target="tpu_custom_call" | custom-call | tf_op jit(solution)/shard_map/panels/pallas_call | solution.py:493
  224.9 1.9 copy.5
